TPU v7x, 32 devices: a whole 2x2x4 slice. The times are simulated.
32 devices in a mesh: data: 2 (over x), time: 16 (over z, y, core).
Axes of the slice: x: 2, y: 2, z: 4, core: 2. Of those that a mesh axis runs over, the one named last changes fastest.
Arguments:
- x_init: float32 [24, 256, 384], P('data'), parts along dimension 0
- w_in: bfloat16 [384, 1536], replicated
- w_out: bfloat16 [1536, 384], replicated
- mod_gamma: bfloat16 [64, 1536], P('time')
- mod_beta: bfloat16 [64, 1536], P('time')
- step_size: float32 [64], P('time')
Outputs:
- output: float32 [24, 256, 384], P('data'), parts along dimension 0
There are 2 independent parts. A program takes and returns all parts, laid end to end along the dimension named above; an argument that names none is the same for every part.
All inputs are finite; a program needn't handle non-finite values.
Results may differ from a plain program's by a relative error of at most 0.001.
Values are sent between devices in bfloat16 or wider.
A program may use at most 1 GiB of HBM per device.

v0:
```python
import jax
import jax.numpy as jnp
from jax import lax
from jax.sharding import PartitionSpec as P

SWEEPS = 4


def solution(mesh):
    groups = mesh.shape["time"]
    distances = [2 ** level for level in range(12) if 2 ** level < groups]

    def prefix_of(own_total):
        prefix = jnp.zeros_like(own_total)
        inclusive = own_total
        for distance in distances:
            send_pairs = [(source, source + distance) for source in range(groups - distance)]
            received = lax.ppermute(inclusive, "time", send_pairs)
            inclusive = inclusive + received
            prefix = prefix + received
        return prefix

    def local_run(x_init, w_in, w_out, mod_gamma, mod_beta, step_size):
        mod_scale = (1.0 + mod_gamma.astype(jnp.float32))[:, None, None, :]
        mod_shift = mod_beta.astype(jnp.float32)[:, None, None, :]
        h_steps = step_size[:, None, None, None]
        pre_act = jnp.einsum("bnc,cd->bnd", x_init.astype(jnp.bfloat16), w_in, preferred_element_type=jnp.float32)[None]
        result = x_init
        for sweep_idx in range(SWEEPS):
            hidden_act = jax.nn.gelu(pre_act * mod_scale + mod_shift, approximate=True).astype(jnp.bfloat16)
            drifts = jnp.einsum("kbnd,dc->kbnc", hidden_act, w_out, preferred_element_type=jnp.float32) * h_steps
            if sweep_idx < SWEEPS - 1:
                running = jnp.cumsum(drifts, axis=0)
                latents = x_init + prefix_of(running[-1]) + (running - drifts)
                pre_act = jnp.einsum("kbnc,cd->kbnd", latents.astype(jnp.bfloat16), w_in, preferred_element_type=jnp.float32)
            else:
                result = x_init + lax.psum(jnp.sum(drifts, axis=0), "time")
        return result

    return jax.shard_map(local_run, mesh=mesh, in_specs=(P("data", None, None), P(None, None), P(None, None), P("time", None), P("time", None), P("time")), out_specs=P("data", None, None), check_vma=False)
```

profile of v0, /device:TPU:1, one launch (start us, length us, event | category | flops | bytes accessed | tf_op | source)
XLA Modules:
  0.0 1911.0 jit_solution(2186495866193958761)
XLA Ops:
  6.5 0.0 copy-start
  6.5 0.0 all-reduce.2.cloned.1.call-start
  6.5 0.8 convert_add_fusion
  7.3 0.7 convert_element_type.32
  8.1 0.0 copy-done
  8.1 7.1 fusion.67
  15.1 0.0 copy-done.11
  15.2 0.0 copy-start.10
  15.2 31.8 %fusion.32 = f32[4,12,256,384]{3,2,1,0:T(8,128)} fusion(f32[4,1536]{1,0:T(4,128)S(1)} %convert_element_type.32, f32[4,1536]{1,0:T(4,128)S(1)} %convert_add_fusion, f32[12,256,1536]{2,1,0:T(8,128)S(1)} %fusion.67, bf16[1536,384]{1,0:T(8,128)(2,1)S(1)} %copy-done.11), kind=kOutput, calls=%fused_computation.36 | convolution fusion | flops 14703132672 | bytes 38977536 | tf_op jit(solution)/shard_map/kbnd,dc->kbnc/dot_general | solution.py:31
  47.0 0.0 copy-done.10
  47.0 15.1 fusion.44
  62.0 2.6 slice_bitcast_fusion.2
  64.7 4.5 collective-permute-start
  69.2 51.0 %collective-permute-done = f32[12,256,384]{2,1,0:T(8,128)S(1)} collective-permute-done((f32[12,256,384]{2,1,0:T(8,128)S(1)}, f32[12,256,384]{2,1,0:T(8,128)S(1)}, u32[]{:S(2)}, u32[]{:S(2)}) %collective-permute-start) | collective-permute-done | bytes 4718624 | tf_op jit(solution)/shard_map/ppermute | solution.py:18
  120.2 4.7 fusion.98
  124.9 3.4 collective-permute-start.1
  128.4 99.5 %collective-permute-done.1 = f32[12,256,384]{2,1,0:T(8,128)S(1)} collective-permute-done((f32[12,256,384]{2,1,0:T(8,128)S(1)}, f32[12,256,384]{2,1,0:T(8,128)S(1)}, u32[]{:S(2)}, u32[]{:S(2)}) %collective-permute-start.1) | collective-permute-done | bytes 4718624 | tf_op jit(solution)/shard_map/ppermute | solution.py:18
  227.8 0.5 add.156
  228.3 4.5 collective-permute-start.2
  232.8 97.5 %collective-permute-done.2 = f32[12,256,384]{2,1,0:T(8,128)S(1)} collective-permute-done((f32[12,256,384]{2,1,0:T(8,128)S(1)}, f32[12,256,384]{2,1,0:T(8,128)S(1)}, u32[]{:S(2)}, u32[]{:S(2)}) %collective-permute-start.2) | collective-permute-done | bytes 4718624 | tf_op jit(solution)/shard_map/ppermute | solution.py:18
  330.3 0.5 add.158
  330.7 0.0 copy-done.1
  330.8 7.3 collective-permute-start.3
  338.0 0.0 copy-done.4
  338.0 0.0 copy-done.7
  338.0 95.2 %collective-permute-done.3 = f32[12,256,384]{2,1,0:T(8,128)} collective-permute-done((f32[12,256,384]{2,1,0:T(8,128)S(1)}, f32[12,256,384]{2,1,0:T(8,128)}, u32[]{:S(2)}, u32[]{:S(2)}) %collective-permute-start.3) | collective-permute-done | bytes 4718624 | tf_op jit(solution)/shard_map/ppermute | solution.py:18
  433.2 11.4 add_add_fusion.2
  444.6 45.2 %fusion.115 = bf16[4,12,256,1536]{3,2,1,0:T(8,128)(2,1)} fusion(f32[4,1536]{1,0:T(4,128)S(1)} %convert_element_type.32, f32[4,1536]{1,0:T(4,128)S(1)} %convert_add_fusion, f32[4,12,256,384]{3,2,1,0:T(8,128)} %fusion.44, f32[4,12,256,384]{3,2,1,0:T(8,128)} %fusion.32, f32[12,256,384]{2,1,0:T(8,128)} %add_add_fusion.2, f32[4]{0:T(128)S(1)} %copy-done.10, ...), kind=kOutput, calls=%fused_computation.19.clone.clone | convolution fusion | flops 14722007040 | bytes 81444880 | tf_op jit(solution)/shard_map/kbnc,cd->kbnd/dot_general | solution.py:35
  489.8 27.4 %fusion.38 = f32[4,12,256,384]{3,2,1,0:T(8,128)} fusion(bf16[1536,384]{1,0:T(8,128)(2,1)S(1)} %copy-done.11, bf16[4,12,256,1536]{3,2,1,0:T(8,128)(2,1)} %fusion.115), kind=kOutput, calls=%fused_computation.39 | convolution fusion | flops 14495514624 | bytes 57802752 | tf_op jit(solution)/shard_map/kbnd,dc->kbnc/dot_general | solution.py:31
  517.2 27.3 %fusion.42 = f32[4,12,256,384]{3,2,1,0:T(8,128)} fusion(f32[4,12,256,384]{3,2,1,0:T(8,128)} %fusion.38, f32[4]{0:T(128)S(1)} %copy-done.10), kind=kOutput, calls=%fused_computation.46 | output fusion | flops 18874368 | bytes 37748752 | tf_op jit(solution)/shard_map/jit(cumsum)/reduce_window_sum | solution.py:33
  544.6 2.6 slice_bitcast_fusion.1
  547.2 9.5 collective-permute-start.4
  556.7 51.0 %collective-permute-done.4 = f32[12,256,384]{2,1,0:T(8,128)S(1)} collective-permute-done((f32[12,256,384]{2,1,0:T(8,128)S(1)}, f32[12,256,384]{2,1,0:T(8,128)S(1)}, u32[]{:S(2)}, u32[]{:S(2)}) %collective-permute-start.4) | collective-permute-done | bytes 4718624 | tf_op jit(solution)/shard_map/ppermute | solution.py:18
  607.8 4.7 fusion.99
  612.4 102.6 %collective-permute-start.5 = (f32[12,256,384]{2,1,0:T(8,128)S(1)}, f32[12,256,384]{2,1,0:T(8,128)S(1)}, u32[]{:S(2)}, u32[]{:S(2)}) collective-permute-start(f32[12,256,384]{2,1,0:T(8,128)S(1)} %fusion.99), channel_id=1, source_target_pairs={{0,2},{1,3},{2,4},{3,5},{4,6},{5,7},{6,8},{7,9},{8,10},{9,11},{10,... | collective-permute-start | bytes 14155784 | tf_op jit(solution)/shard_map/ppermute | solution.py:18
  715.0 50.7 %collective-permute-done.5 = f32[12,256,384]{2,1,0:T(8,128)S(1)} collective-permute-done((f32[12,256,384]{2,1,0:T(8,128)S(1)}, f32[12,256,384]{2,1,0:T(8,128)S(1)}, u32[]{:S(2)}, u32[]{:S(2)}) %collective-permute-start.5) | collective-permute-done | bytes 4718624 | tf_op jit(solution)/shard_map/ppermute | solution.py:18
  765.7 0.5 add.168
  766.2 53.1 %collective-permute-start.6 = (f32[12,256,384]{2,1,0:T(8,128)S(1)}, f32[12,256,384]{2,1,0:T(8,128)S(1)}, u32[]{:S(2)}, u32[]{:S(2)}) collective-permute-start(f32[12,256,384]{2,1,0:T(8,128)S(1)} %add.168), channel_id=1, source_target_pairs={{0,4},{1,5},{2,6},{3,7},{4,8},{5,9},{6,10},{7,11},{8,12},{9,13},{1... | collective-permute-start | bytes 14155784 | tf_op jit(solution)/shard_map/ppermute | solution.py:18
  819.3 97.4 %collective-permute-done.6 = f32[12,256,384]{2,1,0:T(8,128)S(1)} collective-permute-done((f32[12,256,384]{2,1,0:T(8,128)S(1)}, f32[12,256,384]{2,1,0:T(8,128)S(1)}, u32[]{:S(2)}, u32[]{:S(2)}) %collective-permute-start.6) | collective-permute-done | bytes 4718624 | tf_op jit(solution)/shard_map/ppermute | solution.py:18
  916.7 0.5 add.170
  917.2 7.5 collective-permute-start.7
  924.6 95.3 %collective-permute-done.7 = f32[12,256,384]{2,1,0:T(8,128)} collective-permute-done((f32[12,256,384]{2,1,0:T(8,128)S(1)}, f32[12,256,384]{2,1,0:T(8,128)}, u32[]{:S(2)}, u32[]{:S(2)}) %collective-permute-start.7) | collective-permute-done | bytes 4718624 | tf_op jit(solution)/shard_map/ppermute | solution.py:18
  1020.0 11.4 add_add_fusion.1
  1031.4 44.8 %fusion.112 = bf16[4,12,256,1536]{3,2,1,0:T(8,128)(2,1)} fusion(f32[4,1536]{1,0:T(4,128)S(1)} %convert_element_type.32, f32[4,1536]{1,0:T(4,128)S(1)} %convert_add_fusion, f32[4,12,256,384]{3,2,1,0:T(8,128)} %fusion.42, f32[4,12,256,384]{3,2,1,0:T(8,128)} %fusion.38, f32[12,256,384]{2,1,0:T(8,128)} %add_add_fusion.1, f32[4]{0:T(128)S(1)} %copy-done.10, ...), kind=kOutput, calls=%fused_computation.27.clone.clone.1 | convolution fusion | flops 14722007040 | bytes 81444880 | tf_op jit(solution)/shard_map/kbnc,cd->kbnd/dot_general | solution.py:35
  1076.2 27.4 %fusion.36 = f32[4,12,256,384]{3,2,1,0:T(8,128)} fusion(bf16[1536,384]{1,0:T(8,128)(2,1)S(1)} %copy-done.11, bf16[4,12,256,1536]{3,2,1,0:T(8,128)(2,1)} %fusion.112), kind=kOutput, calls=%fused_computation.38 | convolution fusion | flops 14495514624 | bytes 57802752 | tf_op jit(solution)/shard_map/kbnd,dc->kbnc/dot_general | solution.py:31
  1103.6 15.2 fusion.40
  1118.9 2.6 slice_bitcast_fusion
  1121.5 9.1 collective-permute-start.8
  1130.6 51.0 %collective-permute-done.8 = f32[12,256,384]{2,1,0:T(8,128)S(1)} collective-permute-done((f32[12,256,384]{2,1,0:T(8,128)S(1)}, f32[12,256,384]{2,1,0:T(8,128)S(1)}, u32[]{:S(2)}, u32[]{:S(2)}) %collective-permute-start.8) | collective-permute-done | bytes 4718624 | tf_op jit(solution)/shard_map/ppermute | solution.py:18
  1181.6 4.7 fusion.100
  1186.3 102.8 %collective-permute-start.9 = (f32[12,256,384]{2,1,0:T(8,128)S(1)}, f32[12,256,384]{2,1,0:T(8,128)S(1)}, u32[]{:S(2)}, u32[]{:S(2)}) collective-permute-start(f32[12,256,384]{2,1,0:T(8,128)S(1)} %fusion.100), channel_id=1, source_target_pairs={{0,2},{1,3},{2,4},{3,5},{4,6},{5,7},{6,8},{7,9},{8,10},{9,11},{10,... | collective-permute-start | bytes 14155784 | tf_op jit(solution)/shard_map/ppermute | solution.py:18
  1289.1 50.7 %collective-permute-done.9 = f32[12,256,384]{2,1,0:T(8,128)S(1)} collective-permute-done((f32[12,256,384]{2,1,0:T(8,128)S(1)}, f32[12,256,384]{2,1,0:T(8,128)S(1)}, u32[]{:S(2)}, u32[]{:S(2)}) %collective-permute-start.9) | collective-permute-done | bytes 4718624 | tf_op jit(solution)/shard_map/ppermute | solution.py:18
  1339.8 0.5 add.180
  1340.3 51.1 %collective-permute-start.10 = (f32[12,256,384]{2,1,0:T(8,128)S(1)}, f32[12,256,384]{2,1,0:T(8,128)S(1)}, u32[]{:S(2)}, u32[]{:S(2)}) collective-permute-start(f32[12,256,384]{2,1,0:T(8,128)S(1)} %add.180), channel_id=1, source_target_pairs={{0,4},{1,5},{2,6},{3,7},{4,8},{5,9},{6,10},{7,11},{8,12},{9,13},{1... | collective-permute-start | bytes 14155784 | tf_op jit(solution)/shard_map/ppermute | solution.py:18
  1391.4 96.4 %collective-permute-done.10 = f32[12,256,384]{2,1,0:T(8,128)S(1)} collective-permute-done((f32[12,256,384]{2,1,0:T(8,128)S(1)}, f32[12,256,384]{2,1,0:T(8,128)S(1)}, u32[]{:S(2)}, u32[]{:S(2)}) %collective-permute-start.10) | collective-permute-done | bytes 4718624 | tf_op jit(solution)/shard_map/ppermute | solution.py:18
  1487.8 0.5 add.182
  1488.3 7.9 collective-permute-start.11
  1496.2 94.8 %collective-permute-done.11 = f32[12,256,384]{2,1,0:T(8,128)} collective-permute-done((f32[12,256,384]{2,1,0:T(8,128)S(1)}, f32[12,256,384]{2,1,0:T(8,128)}, u32[]{:S(2)}, u32[]{:S(2)}) %collective-permute-start.11) | collective-permute-done | bytes 4718624 | tf_op jit(solution)/shard_map/ppermute | solution.py:18
  1591.0 11.4 add_add_fusion
  1602.5 45.2 %fusion.118 = bf16[4,12,256,1536]{3,2,1,0:T(8,128)(2,1)} fusion(f32[4,1536]{1,0:T(4,128)S(1)} %convert_element_type.32, f32[4,1536]{1,0:T(4,128)S(1)} %convert_add_fusion, f32[4,12,256,384]{3,2,1,0:T(8,128)} %fusion.40, f32[4,12,256,384]{3,2,1,0:T(8,128)} %fusion.36, f32[12,256,384]{2,1,0:T(8,128)} %add_add_fusion, ...), kind=kOutput, calls=%fused_computation.35.clone.clone.clone.clone.1 | convolution fusion | flops 14722007040 | bytes 81444880 | tf_op jit(solution)/shard_map/kbnc,cd->kbnd/dot_general | solution.py:35
  1647.6 27.4 %multiply_reduce_fusion = f32[12,256,384]{2,1,0:T(8,128)} fusion(f32[4]{0:T(128)S(1)} %copy-done.10, bf16[1536,384]{1,0:T(8,128)(2,1)S(1)} %copy-done.11, bf16[4,12,256,1536]{3,2,1,0:T(8,128)(2,1)} %fusion.118), kind=kOutput, calls=%fused_computation.40 | convolution fusion | flops 14503772160 | bytes 43646992 | tf_op jit(solution)/shard_map/kbnd,dc->kbnc/dot_general | solution.py:31
  1675.1 0.0 all-reduce.2.cloned.1.call-update
  1675.1 222.4 %all-reduce.2.cloned.1.call-done = f32[12,256,384]{2,1,0:T(8,128)} async-done(((f32[12,256,384]{2,1,0:T(8,128)}), f32[12,256,384]{2,1,0:T(8,128)}) %all-reduce.2.cloned.1.call-update) | async-done | bytes 4718608 | tf_op jit(solution)/shard_map/psum | solution.py:37
  1897.5 6.4 add.190
  (16 shorter events, 0.0 us)
Async XLA Ops:
  6.5 1.5 copy-start
  6.5 1891.0 %all-reduce.2.cloned.1.call-start = ((), (), s32[]{:S(2)}) async-start(), calls=%async_computation | async-start | bytes 9437184 | tf_op jit(solution)/shard_map/psum | solution.py:37
  8.1 7.1 copy-start.11
  15.2 31.8 %copy-start.10 = (f32[4]{0:T(128)S(1)}, f32[4]{0:T(128)}, u32[]{:S(2)}) copy-start(f32[4]{0:T(128)} %param.11) | copy-start | bytes 52
  64.7 55.6 %collective-permute-start = (f32[12,256,384]{2,1,0:T(8,128)S(1)}, f32[12,256,384]{2,1,0:T(8,128)S(1)}, u32[]{:S(2)}, u32[]{:S(2)}) collective-permute-start(f32[12,256,384]{2,1,0:T(8,128)S(1)} %slice_bitcast_fusion.2), channel_id=1, source_target_pairs={{0,1},{1,2},{2,3},{3,4},{4,5},{5,6},{6,7},{7,8},{8,9},{9,10},{10,1... | collective-permute-start | bytes 14155784 | tf_op jit(solution)/shard_map/ppermute | solution.py:18
  120.2 210.5 %copy-start.1 = (f32[12,256,384]{2,1,0:T(8,128)}, f32[12,256,384]{2,1,0:T(8,128)S(1)}, u32[]{:S(2)}) copy-start(f32[12,256,384]{2,1,0:T(8,128)S(1)} %collective-permute-done) | copy-start | bytes 14155780
  124.9 102.9 %collective-permute-start.1 = (f32[12,256,384]{2,1,0:T(8,128)S(1)}, f32[12,256,384]{2,1,0:T(8,128)S(1)}, u32[]{:S(2)}, u32[]{:S(2)}) collective-permute-start(f32[12,256,384]{2,1,0:T(8,128)S(1)} %fusion.98), channel_id=1, source_target_pairs={{0,2},{1,3},{2,4},{3,5},{4,6},{5,7},{6,8},{7,9},{8,10},{9,11},{10,... | collective-permute-start | bytes 14155784 | tf_op jit(solution)/shard_map/ppermute | solution.py:18
  227.8 110.2 %copy-start.4 = (f32[12,256,384]{2,1,0:T(8,128)}, f32[12,256,384]{2,1,0:T(8,128)S(1)}, u32[]{:S(2)}) copy-start(f32[12,256,384]{2,1,0:T(8,128)S(1)} %collective-permute-done.1) | copy-start | bytes 14155780
  228.3 102.0 %collective-permute-start.2 = (f32[12,256,384]{2,1,0:T(8,128)S(1)}, f32[12,256,384]{2,1,0:T(8,128)S(1)}, u32[]{:S(2)}, u32[]{:S(2)}) collective-permute-start(f32[12,256,384]{2,1,0:T(8,128)S(1)} %add.156), channel_id=1, source_target_pairs={{0,4},{1,5},{2,6},{3,7},{4,8},{5,9},{6,10},{7,11},{8,12},{9,13},{1... | collective-permute-start | bytes 14155784 | tf_op jit(solution)/shard_map/ppermute | solution.py:18
  330.3 7.8 copy-start.7
  330.8 102.4 %collective-permute-start.3 = (f32[12,256,384]{2,1,0:T(8,128)S(1)}, f32[12,256,384]{2,1,0:T(8,128)}, u32[]{:S(2)}, u32[]{:S(2)}) collective-permute-start(f32[12,256,384]{2,1,0:T(8,128)S(1)} %add.158), channel_id=1, source_target_pairs={{0,8},{1,9},{2,10},{3,11},{4,12},{5,13},{6,14},{7,15},{16,24},{17,... | collective-permute-start | bytes 14155784 | tf_op jit(solution)/shard_map/ppermute | solution.py:18
  547.2 60.5 %collective-permute-start.4 = (f32[12,256,384]{2,1,0:T(8,128)S(1)}, f32[12,256,384]{2,1,0:T(8,128)S(1)}, u32[]{:S(2)}, u32[]{:S(2)}) collective-permute-start(f32[12,256,384]{2,1,0:T(8,128)S(1)} %slice_bitcast_fusion.1), channel_id=1, source_target_pairs={{0,1},{1,2},{2,3},{3,4},{4,5},{5,6},{6,7},{7,8},{8,9},{9,10},{10,1... | collective-permute-start | bytes 14155784 | tf_op jit(solution)/shard_map/ppermute | solution.py:18
  607.7 309.4 %copy-start.2 = (f32[12,256,384]{2,1,0:T(8,128)}, f32[12,256,384]{2,1,0:T(8,128)S(1)}, u32[]{:S(2)}) copy-start(f32[12,256,384]{2,1,0:T(8,128)S(1)} %collective-permute-done.4) | copy-start | bytes 14155780
  612.4 153.3 %collective-permute-start.5 = (f32[12,256,384]{2,1,0:T(8,128)S(1)}, f32[12,256,384]{2,1,0:T(8,128)S(1)}, u32[]{:S(2)}, u32[]{:S(2)}) collective-permute-start(f32[12,256,384]{2,1,0:T(8,128)S(1)} %fusion.99), channel_id=1, source_target_pairs={{0,2},{1,3},{2,4},{3,5},{4,6},{5,7},{6,8},{7,9},{8,10},{9,11},{10,... | collective-permute-start | bytes 14155784 | tf_op jit(solution)/shard_map/ppermute | solution.py:18
  765.7 158.9 %copy-start.5 = (f32[12,256,384]{2,1,0:T(8,128)}, f32[12,256,384]{2,1,0:T(8,128)S(1)}, u32[]{:S(2)}) copy-start(f32[12,256,384]{2,1,0:T(8,128)S(1)} %collective-permute-done.5) | copy-start | bytes 14155780
  766.2 150.4 %collective-permute-start.6 = (f32[12,256,384]{2,1,0:T(8,128)S(1)}, f32[12,256,384]{2,1,0:T(8,128)S(1)}, u32[]{:S(2)}, u32[]{:S(2)}) collective-permute-start(f32[12,256,384]{2,1,0:T(8,128)S(1)} %add.168), channel_id=1, source_target_pairs={{0,4},{1,5},{2,6},{3,7},{4,8},{5,9},{6,10},{7,11},{8,12},{9,13},{1... | collective-permute-start | bytes 14155784 | tf_op jit(solution)/shard_map/ppermute | solution.py:18
  916.7 8.0 copy-start.8
  917.2 102.8 %collective-permute-start.7 = (f32[12,256,384]{2,1,0:T(8,128)S(1)}, f32[12,256,384]{2,1,0:T(8,128)}, u32[]{:S(2)}, u32[]{:S(2)}) collective-permute-start(f32[12,256,384]{2,1,0:T(8,128)S(1)} %add.170), channel_id=1, source_target_pairs={{0,8},{1,9},{2,10},{3,11},{4,12},{5,13},{6,14},{7,15},{16,24},{17,... | collective-permute-start | bytes 14155784 | tf_op jit(solution)/shard_map/ppermute | solution.py:18
  1121.5 60.1 %collective-permute-start.8 = (f32[12,256,384]{2,1,0:T(8,128)S(1)}, f32[12,256,384]{2,1,0:T(8,128)S(1)}, u32[]{:S(2)}, u32[]{:S(2)}) collective-permute-start(f32[12,256,384]{2,1,0:T(8,128)S(1)} %slice_bitcast_fusion), channel_id=1, source_target_pairs={{0,1},{1,2},{2,3},{3,4},{4,5},{5,6},{6,7},{7,8},{8,9},{9,10},{10,1... | collective-permute-start | bytes 14155784 | tf_op jit(solution)/shard_map/ppermute | solution.py:18
  1181.6 306.7 %copy-start.3 = (f32[12,256,384]{2,1,0:T(8,128)}, f32[12,256,384]{2,1,0:T(8,128)S(1)}, u32[]{:S(2)}) copy-start(f32[12,256,384]{2,1,0:T(8,128)S(1)} %collective-permute-done.8) | copy-start | bytes 14155780
  1186.3 153.6 %collective-permute-start.9 = (f32[12,256,384]{2,1,0:T(8,128)S(1)}, f32[12,256,384]{2,1,0:T(8,128)S(1)}, u32[]{:S(2)}, u32[]{:S(2)}) collective-permute-start(f32[12,256,384]{2,1,0:T(8,128)S(1)} %fusion.100), channel_id=1, source_target_pairs={{0,2},{1,3},{2,4},{3,5},{4,6},{5,7},{6,8},{7,9},{8,10},{9,11},{10,... | collective-permute-start | bytes 14155784 | tf_op jit(solution)/shard_map/ppermute | solution.py:18
  1339.8 156.4 %copy-start.6 = (f32[12,256,384]{2,1,0:T(8,128)}, f32[12,256,384]{2,1,0:T(8,128)S(1)}, u32[]{:S(2)}) copy-start(f32[12,256,384]{2,1,0:T(8,128)S(1)} %collective-permute-done.9) | copy-start | bytes 14155780
  1340.3 147.4 %collective-permute-start.10 = (f32[12,256,384]{2,1,0:T(8,128)S(1)}, f32[12,256,384]{2,1,0:T(8,128)S(1)}, u32[]{:S(2)}, u32[]{:S(2)}) collective-permute-start(f32[12,256,384]{2,1,0:T(8,128)S(1)} %add.180), channel_id=1, source_target_pairs={{0,4},{1,5},{2,6},{3,7},{4,8},{5,9},{6,10},{7,11},{8,12},{9,13},{1... | collective-permute-start | bytes 14155784 | tf_op jit(solution)/shard_map/ppermute | solution.py:18
  1487.8 8.4 copy-start.9
  1488.3 102.8 %collective-permute-start.11 = (f32[12,256,384]{2,1,0:T(8,128)S(1)}, f32[12,256,384]{2,1,0:T(8,128)}, u32[]{:S(2)}, u32[]{:S(2)}) collective-permute-start(f32[12,256,384]{2,1,0:T(8,128)S(1)} %add.182), channel_id=1, source_target_pairs={{0,8},{1,9},{2,10},{3,11},{4,12},{5,13},{6,14},{7,15},{16,24},{17,... | collective-permute-start | bytes 14155784 | tf_op jit(solution)/shard_map/ppermute | solution.py:18
Sparse Core Ops, SparseCore 0:
  1675.2 222.2 all-reduce.1
where the time goes:
time: 1920 us; the launch traced here: 1910 us
  waiting for transfers between devices  1150 us (60%)
  starting transfers between devices  363 us (19%)
  matrix products  256 us (13%)
  other arithmetic  117 us (6%)
    ppermute x12, waiting for transfers between devices, prefix_of(): received = lax.ppermute(inclusive, 'time', send_pairs)  931 us
    ppermute x12, starting transfers between devices, prefix_of(): received = lax.ppermute(inclusive, 'time', send_pairs)  363 us
    psum x1, waiting for transfers between devices, local_run(): result = x_init + lax.psum(jnp.sum(drifts, axis=0), 'time')  222 us
    dot_general x3, matrix products, local_run(): jnp.einsum('kbnc,cd->kbnd', latents.astype(jnp.bfloat16), w_in, preferred...  135 us
    dot_general x4, matrix products, local_run(): jnp.einsum('kbnd,dc->kbnc', hidden_act, w_out, preferred_element_type=jnp...  114 us
    another operation x3, other arithmetic, local_run(): running = jnp.cumsum(drifts, axis=0)  57.6 us
  transfers between devices with their start and end apart: 13, of which 13 were waited for; matrix products, arithmetic and copies ran while one was open for 0% of the time, Pallas kernels for 0%

commit v1 on v0

v1 whole, which is shorter than its diff:
```python
import functools
import math

import jax
import jax.numpy as jnp
from jax import lax
from jax.experimental import pallas as pl
from jax.experimental.pallas import tpu as pltpu
from jax.sharding import PartitionSpec as P

PASSES = 2
OWN = 4
DEVS = 16
STEPS = OWN * DEVS
BLOCKS = DEVS + -(-3 // OWN)
TILE = 256
C0 = math.sqrt(2.0 / math.pi)
K0 = 2.0 * C0
K1 = 8.0 * C0 * 0.044715


def _sampler(x_ref, win_ref, wout_ref, gam_ref, bet_ref, h_ref, y_ref,
             x_s, gam_all, bet_all, h_all, scale, shift, h_row, a0, run, total,
             xb, hid, y_all,
             x_sem, out_sem, ms, mr, zs, zr, ys, yr, cs, cr):
    every = x_s.shape[0]
    first = every * 2 // 3
    spans = ((0, first), (first, every - first))
    hidden = a0.shape[1]
    tiles = [pl.ds(i * TILE, TILE) for i in range(hidden // TILE)]
    me = lax.axis_index("time")
    z = me // 4
    y = (me // 2) % 2
    c = me % 2

    def dev(zz, yy, cc):
        return zz * 4 + yy * 2 + cc

    barrier = pltpu.get_barrier_semaphore()
    for d in range(1, DEVS):
        pl.semaphore_signal(barrier, inc=1, device_id={"time": lax.rem(me + d, DEVS)},
                            device_id_type=pl.DeviceIdType.MESH)
    x_copy = pltpu.make_async_copy(
        x_ref.at[me], x_s, x_sem)
    x_copy.start()
    gam_all[me] = gam_ref[...]
    bet_all[me] = bet_ref[...]
    h_all[me] = h_ref[...]
    pl.semaphore_wait(barrier, DEVS - 1)

    def mod_copies(d, owner, peer):
        pairs = ((gam_ref, gam_all), (bet_ref, bet_all), (h_ref, h_all))
        return [pltpu.make_async_remote_copy(
            src_ref=src, dst_ref=dst.at[owner], send_sem=ms.at[d, i],
            recv_sem=mr.at[owner, i], device_id={"time": peer},
            device_id_type=pl.DeviceIdType.MESH)
            for i, (src, dst) in enumerate(pairs)]

    def send_mods():
        def one(d, carry):
            for copy in mod_copies(d, me, lax.rem(me + d, DEVS)):
                copy.start()
            return carry
        lax.fori_loop(1, DEVS, one, 0)

    def take_mods(b):
        @pl.when(b != me)
        def _():
            for copy in mod_copies(0, b, me):
                copy.wait_recv()
        for k in range(OWN):
            scale[b * OWN + k] = 0.5 * (1.0 + gam_all[b, k:k + 1, :].astype(jnp.float32))
            shift[b * OWN + k] = 0.5 * bet_all[b, k:k + 1, :].astype(jnp.float32)
            h_row[b * OWN + k] = h_all[b, k:k + 1, :]

    def block_copy(p, block, peer, send, recv):
        span = pl.ds(*spans[p])
        return pltpu.make_async_remote_copy(
            src_ref=y_all.at[block, span], dst_ref=y_all.at[block, span],
            send_sem=send, recv_sem=recv, device_id={"time": peer},
            device_id_type=pl.DeviceIdType.MESH)

    def z_send(p, d):
        return block_copy(p, me, dev(lax.rem(z + d, 4), y, c), zs.at[p, d - 1], zr.at[p, d - 1])

    def z_recv(p, d):
        return block_copy(p, dev(lax.rem(z + 4 - d, 4), y, c), me, zs.at[p, d - 1], zr.at[p, d - 1])

    def y_send(p, k):
        return block_copy(p, dev(lax.rem(z + 4 - k, 4), y, c), dev(z, 1 - y, c), ys.at[p, k], yr.at[p, k])

    def y_recv(p, k):
        return block_copy(p, dev(lax.rem(z + 4 - k, 4), 1 - y, c), me, ys.at[p, k], yr.at[p, k])

    def c_block(k, cc):
        yy = y if k < 4 else 1 - y
        return dev(lax.rem(z + 4 - k % 4, 4), yy, cc)

    def c_send(p, k):
        return block_copy(p, c_block(k, c), dev(z, y, 1 - c), cs.at[p, k], cr.at[p, k])

    def c_recv(p, k):
        return block_copy(p, c_block(k, 1 - c), me, cs.at[p, k], cr.at[p, k])

    def gather_first(p):
        for d in (1, 3, 2):
            z_send(p, d).start()
        y_send(p, 0).start()
        c_send(p, 0).start()

    def gather_second(p):
        for d in (1, 3, 2):
            z_recv(p, d).wait_recv()
            y_send(p, d).start()
            c_send(p, d).start()

    def gather_third(p):
        for k in (0, 1, 3, 2):
            y_recv(p, k).wait_recv()
            c_send(p, 4 + k).start()

    def out_copy(p):
        span = pl.ds(*spans[p])
        return pltpu.make_async_copy(y_all.at[:, span], y_ref.at[:, span], out_sem.at[p])

    def gather_last(p):
        for k in range(8):
            c_recv(p, k).wait_recv()
        out_copy(p).start()

    @pl.when(me < 2)
    def _():
        send_mods()

    x_copy.wait()

    def body(p, n):
        rows = spans[p][1]
        x0 = x_s[pl.ds(*spans[p])]
        for s in range(3):
            xb[s * rows:(s + 1) * rows, :] = (x0 + run[s, 0:rows]).astype(jnp.bfloat16)
        acc = None
        steps = [n - s for s in range(4)]
        index = [jnp.clip(j, 0, STEPS - 1) for j in steps]
        for t in tiles:
            part = jnp.dot(hid[0:3 * rows, t], wout_ref[t, :], preferred_element_type=jnp.float32)
            acc = part if acc is None else acc + part
            pre = jnp.dot(xb[0:3 * rows, :], win_ref[:, t], preferred_element_type=jnp.float32)
            for s in range(4):
                a = a0[0:rows, t] if s == 0 else pre[(s - 1) * rows:s * rows, :]
                v = a * scale[index[s], :, t] + shift[index[s], :, t]
                g = (v + v * jnp.tanh(v * (K1 * (v * v) + K0))).astype(jnp.bfloat16)
                if s < 3:
                    hid[s * rows:(s + 1) * rows, t] = g
                else:
                    term = h_row[index[s], :, 0:TILE] * g.astype(jnp.float32)
                    good = jnp.logical_and(steps[s] >= 0, steps[s] < STEPS)
                    total[0:rows, t] += jnp.where(good, term, 0.0)
        for s in range(3):
            j = n - 1 - s
            good = jnp.logical_and(j >= 0, j < STEPS)
            term = h_row[jnp.clip(j, 0, STEPS - 1)] * acc[s * rows:(s + 1) * rows, :]
            run[s, 0:rows] = run[s, 0:rows] + jnp.where(good, term, 0.0)

    for p in range(PASSES):
        rows = spans[p][1]
        run[...] = jnp.zeros_like(run)
        total[...] = jnp.zeros_like(total)
        hid[...] = jnp.zeros_like(hid)
        xb[0:rows, :] = x_s[pl.ds(*spans[p])].astype(jnp.bfloat16)
        for t in tiles:
            a0[0:rows, t] = jnp.dot(xb[0:rows, :], win_ref[:, t], preferred_element_type=jnp.float32)

        def block(b, carry, p=p):
            if p == 0:
                @pl.when(b + 2 == me)
                def _():
                    send_mods()

                @pl.when(b < DEVS)
                def _():
                    take_mods(b)
            else:
                for at, stage in ((7, gather_second), (13, gather_third), (16, gather_last)):
                    @pl.when(b == at)
                    def _(stage=stage):
                        stage(p - 1)

            def inner(k, carry):
                body(p, b * OWN + k)
                return carry
            lax.fori_loop(0, OWN, inner, 0, unroll=OWN)
            return carry

        lax.fori_loop(0, BLOCKS, block, 0)

        for t in tiles:
            rest = total[0:rows, t]
            for s in range(3):
                part = rest.astype(jnp.bfloat16)
                hid[s * rows:(s + 1) * rows, t] = part
                rest = rest - part.astype(jnp.float32)
        out = jnp.dot(hid[0:3 * rows, :], wout_ref[...], preferred_element_type=jnp.float32)
        out = out[0:rows] + (out[rows:2 * rows] + out[2 * rows:3 * rows])
        y_all[me, pl.ds(*spans[p])] = x_s[pl.ds(*spans[p])] + out
        gather_first(p)

    last = PASSES - 1
    gather_second(last)
    gather_third(last)
    gather_last(last)
    for p in range(PASSES):
        for d in range(1, 4):
            z_send(p, d).wait_send()
        for k in range(4):
            y_send(p, k).wait_send()
        for k in range(8):
            c_send(p, k).wait_send()

    def sent(d, carry):
        for copy in mod_copies(d, me, lax.rem(me + d, DEVS)):
            copy.wait_send()
        return carry
    lax.fori_loop(1, DEVS, sent, 0)
    for p in range(PASSES):
        out_copy(p).wait()


def solution(mesh):
    assert mesh.shape["time"] == DEVS

    def local_run(x_init, w_in, w_out, mod_gamma, mod_beta, step_size):
        channels, hidden = w_in.shape
        every = x_init.size // channels // DEVS
        rows = every * 2 // 3
        x_rows = x_init.reshape(DEVS, every, channels)
        h_wide = jnp.broadcast_to(step_size[:, None], (OWN, channels))
        vmem = pl.BlockSpec(memory_space=pltpu.VMEM)
        dma = pltpu.SemaphoreType.DMA
        f32, bf16 = jnp.float32, jnp.bfloat16
        y = pl.pallas_call(
            _sampler,
            out_shape=jax.ShapeDtypeStruct((DEVS, every, channels), f32),
            in_specs=[pl.BlockSpec(memory_space=pl.ANY)] + [vmem] * 5,
            out_specs=pl.BlockSpec(memory_space=pl.ANY),
            scratch_shapes=[
                pltpu.VMEM((every, channels), f32),
                pltpu.VMEM((DEVS, OWN, hidden), bf16),
                pltpu.VMEM((DEVS, OWN, hidden), bf16),
                pltpu.VMEM((DEVS, OWN, channels), f32),
                pltpu.VMEM((STEPS, 1, hidden), f32),
                pltpu.VMEM((STEPS, 1, hidden), f32),
                pltpu.VMEM((STEPS, 1, channels), f32),
                pltpu.VMEM((rows, hidden), f32),
                pltpu.VMEM((3, rows, channels), f32),
                pltpu.VMEM((rows, hidden), f32),
                pltpu.VMEM((3 * rows, channels), bf16),
                pltpu.VMEM((3 * rows, hidden), bf16),
                pltpu.VMEM((DEVS, every, channels), f32),
                dma(()), dma((PASSES,)),
                dma((DEVS, 3)), dma((DEVS, 3)),
                dma((PASSES, 3)), dma((PASSES, 3)),
                dma((PASSES, 4)), dma((PASSES, 4)),
                dma((PASSES, 8)), dma((PASSES, 8)),
            ],
            compiler_params=pltpu.CompilerParams(
                collective_id=0, has_side_effects=True, vmem_limit_bytes=48 * 1024 * 1024),
            name="sampler",
        )(x_rows, w_in, w_out, mod_gamma, mod_beta, h_wide)
        return y.reshape(x_init.shape)

    return jax.shard_map(
        local_run, mesh=mesh,
        in_specs=(P("data", None, None), P(None, None), P(None, None),
                  P("time", None), P("time", None), P("time")),
        out_specs=P("data", None, None), check_vma=False)
```

time: 1920 us -> 192 us (0.10)
  waiting for transfers between devices: 1150 us -> 0 us
  starting transfers between devices: 363 us -> 0 us
  matrix products: 256 us -> 0 us
  Pallas kernels: 0 us -> 182 us
  other arithmetic: 117 us -> 0 us
    ppermute x12 -> x0, waiting for transfers between devices: 931 us -> none  [prefix_of(): received = lax.ppermute(inclusive, 'time', send_pairs)]
    ppermute x12 -> x0, starting transfers between devices: 363 us -> none  [prefix_of(): received = lax.ppermute(inclusive, 'time', send_pairs)]
    dot_general x8 -> x0, matrix products: 256 us -> none  [the longest x3 135 us: local_run(): jnp.einsum('kbnc,cd->kbnd', latents.astype(jnp.bfloat16), w_in, preferred...]
    psum x1 -> x0, waiting for transfers between devices: 222 us -> none  [local_run(): result = x_init + lax.psum(jnp.sum(drifts, axis=0), 'time')]
    pallas_call x0 -> x1, Pallas kernels: none -> 182 us  [local_run(): pl.pallas_call(_sampler, out_shape=jax.ShapeDtypeStruct((DEVS, every, cha...]
    add x14 -> x0, other arithmetic: 58.5 us -> none  [the longest x3 34.3 us: local_run(): latents = x_init + prefix_of(running[-1]) + (running - drifts)]
    another operation x3 -> x0, other arithmetic: 57.6 us -> none  [local_run(): running = jnp.cumsum(drifts, axis=0)]
  transfers between devices with their start and end apart: 13 -> 0, of which waited for: 13 -> 0; matrix products, arithmetic and copies ran while one was open for 0% -> 0% of each run, Pallas kernels for 0% -> 0%
where the time goes in v1:
time: 192 us
  Pallas kernels  182 us (95%)
  local copies, waits for them, and re-layouts  9.5 us (5%)
    pallas_call x1, Pallas kernels, local_run(): pl.pallas_call(_sampler, out_shape=jax.ShapeDtypeStruct((DEVS, every, cha...  182 us
    unnamed x9, local copies, waits for them, and re-layouts  8.78 us

profile of v1, /device:TPU:1, one launch (start us, length us, event | category | flops | bytes accessed | tf_op | source)
XLA Modules:
  0.0 191.6 jit_solution(3610417699041583333)
XLA Ops:
  0.0 0.7 broadcast_in_dim.2.h_ref
  0.7 0.0 copy-start
  0.7 1.3 copy-done
  2.0 0.0 copy-start.1
  2.0 1.3 copy-done.1
  3.3 0.0 copy-start.2
  3.3 0.7 copy-done.2
  4.0 0.0 copy-start.3
  4.0 0.7 copy-done.3
  4.7 182.1 %sampler.1 = f32[16,192,384]{2,1,0:T(8,128)} custom-call(f32[16,192,384]{2,1,0:T(8,128)} %bitcast.3, bf16[384,1536]{1,0:T(8,128)(2,1)S(1)} %copy-done, bf16[1536,384]{1,0:T(8,128)(2,1)S(1)} %copy-done.1, bf16[4,1536]{1,0:T(4,128)(2,1)S(1)} %copy-done.2, bf16[4,1536]{1,0:T(4,128)(2,1)S(1)} %copy-done.3, f32[4,384]{1,0:T(4,128)S(1)} %broadcast_in_dim.2.h_ref), custom_call_target="tpu_custom_call" | custom-call | tf_op jit(solution)/shard_map/sampler/pallas_call | solution.py:241
  186.8 4.8 %copy.8 = f32[12,256,384]{2,1,0:T(8,128)} copy(f32[12,256,384]{2,1,0:T(8,128)} %bitcast.2) | data formatting | bytes 9437184
Async XLA Ops:
  0.7 1.3 copy-start
  2.0 1.3 copy-start.1
  3.3 0.7 copy-start.2
  4.0 0.7 copy-start.3

commit v2 on v1

--- a/solution.py
+++ b/solution.py
@@ -12,17 +12,16 @@
 OWN = 4
 DEVS = 16
 STEPS = OWN * DEVS
-BLOCKS = DEVS + -(-3 // OWN)
 TILE = 256
 C0 = math.sqrt(2.0 / math.pi)
 K0 = 2.0 * C0
 K1 = 8.0 * C0 * 0.044715
 
 
-def _sampler(x_ref, win_ref, wout_ref, gam_ref, bet_ref, h_ref, y_ref,
-             x_s, gam_all, bet_all, h_all, scale, shift, h_row, a0, run, total,
+def _sampler(x_ref, win_hbm, wout_hbm, gam_ref, bet_ref, h_ref, y_ref,
+             win_ref, wout_ref, x_s, gam_all, bet_all, h_all, scale, shift, h_row, a0, run, total,
              xb, hid, y_all,
-             x_sem, out_sem, ms, mr, zs, zr, ys, yr, cs, cr):
+             x_sem, w_sem, out_sem, ms, mr, zs, zr, ys, yr, cs, cr):
     every = x_s.shape[0]
     first = every * 2 // 3
     spans = ((0, first), (first, every - first))
@@ -43,6 +42,10 @@
     x_copy = pltpu.make_async_copy(
         x_ref.at[me], x_s, x_sem)
     x_copy.start()
+    w_copies = [pltpu.make_async_copy(src, dst, w_sem.at[i]) for i, (src, dst) in
+                enumerate(((win_hbm, win_ref), (wout_hbm, wout_ref)))]
+    for copy in w_copies:
+        copy.start()
     gam_all[me] = gam_ref[...]
     bet_all[me] = bet_ref[...]
     h_all[me] = h_ref[...]
@@ -133,6 +136,8 @@
         send_mods()
 
     x_copy.wait()
+    for copy in w_copies:
+        copy.wait()
 
     def body(p, n):
         rows = spans[p][1]
@@ -177,11 +182,9 @@
                 def _():
                     send_mods()
 
-                @pl.when(b < DEVS)
-                def _():
-                    take_mods(b)
+                take_mods(b)
             else:
-                for at, stage in ((7, gather_second), (13, gather_third), (16, gather_last)):
+                for at, stage in ((7, gather_second), (13, gather_third)):
                     @pl.when(b == at)
                     def _(stage=stage):
                         stage(p - 1)
@@ -192,7 +195,14 @@
             lax.fori_loop(0, OWN, inner, 0, unroll=OWN)
             return carry
 
-        lax.fori_loop(0, BLOCKS, block, 0)
+        lax.fori_loop(0, DEVS, block, 0)
+        if p > 0:
+            gather_last(p - 1)
+
+        def tail(k, carry, p=p):
+            body(p, STEPS + k)
+            return carry
+        lax.fori_loop(0, 3, tail, 0, unroll=3)
 
         for t in tiles:
             rest = total[0:rows, t]
@@ -241,9 +251,11 @@
         y = pl.pallas_call(
             _sampler,
             out_shape=jax.ShapeDtypeStruct((DEVS, every, channels), f32),
-            in_specs=[pl.BlockSpec(memory_space=pl.ANY)] + [vmem] * 5,
+            in_specs=[pl.BlockSpec(memory_space=pltpu.HBM)] * 3 + [vmem] * 3,
             out_specs=pl.BlockSpec(memory_space=pl.ANY),
             scratch_shapes=[
+                pltpu.VMEM((channels, hidden), bf16),
+                pltpu.VMEM((hidden, channels), bf16),
                 pltpu.VMEM((every, channels), f32),
                 pltpu.VMEM((DEVS, OWN, hidden), bf16),
                 pltpu.VMEM((DEVS, OWN, hidden), bf16),
@@ -257,14 +269,14 @@
                 pltpu.VMEM((3 * rows, channels), bf16),
                 pltpu.VMEM((3 * rows, hidden), bf16),
                 pltpu.VMEM((DEVS, every, channels), f32),
-                dma(()), dma((PASSES,)),
+                dma(()), dma((2,)), dma((PASSES,)),
                 dma((DEVS, 3)), dma((DEVS, 3)),
                 dma((PASSES, 3)), dma((PASSES, 3)),
                 dma((PASSES, 4)), dma((PASSES, 4)),
                 dma((PASSES, 8)), dma((PASSES, 8)),
             ],
             compiler_params=pltpu.CompilerParams(
-                collective_id=0, has_side_effects=True, vmem_limit_bytes=48 * 1024 * 1024),
+                collective_id=0, has_side_effects=True, vmem_limit_bytes=67_000_000),
             name="sampler",
         )(x_rows, w_in, w_out, mod_gamma, mod_beta, h_wide)
         return y.reshape(x_init.shape)

time: 192 us -> 186 us (0.969)
  local copies, waits for them, and re-layouts: 9.5 us -> 6.14 us
  Pallas kernels: 182 us -> 180 us
    unnamed x9 -> x1, local copies, waits for them, and re-layouts: 8.78 us -> 4.83 us
    pallas_call x1, Pallas kernels: 182 us -> 180 us  [local_run(): pl.pallas_call(_sampler, out_shape=jax.ShapeDtypeStruct((DEVS, every, cha...]
where the time goes in v2:
time: 186 us
  Pallas kernels  180 us (97%)
  local copies, waits for them, and re-layouts  6.14 us (3%)
    pallas_call x1, Pallas kernels, local_run(): pl.pallas_call(_sampler, out_shape=jax.ShapeDtypeStruct((DEVS, every, cha...  180 us
    unnamed x1, local copies, waits for them, and re-layouts  4.83 us

profile of v2, /device:TPU:1, one launch (start us, length us, event | category | flops | bytes accessed | tf_op | source)
XLA Modules:
  0.0 186.0 jit_solution(6137095349639539549)
XLA Ops:
  0.0 1.3 broadcast_in_dim.2.h_ref
  1.3 179.9 %sampler.1 = f32[16,192,384]{2,1,0:T(8,128)} custom-call(f32[16,192,384]{2,1,0:T(8,128)} %bitcast.3, bf16[384,1536]{1,0:T(8,128)(2,1)} %win_hbm.1, bf16[1536,384]{1,0:T(8,128)(2,1)} %wout_hbm.1, bf16[4,1536]{1,0:T(4,128)(2,1)} %gam_ref.1, bf16[4,1536]{1,0:T(4,128)(2,1)} %bet_ref.1, f32[4,384]{1,0:T(4,128)} %broadcast_in_dim.2.h_ref), custom_call_target="tpu_custom_call" | custom-call | tf_op jit(solution)/shard_map/sampler/pallas_call | solution.py:251
  181.2 4.8 %copy.8 = f32[12,256,384]{2,1,0:T(8,128)} copy(f32[12,256,384]{2,1,0:T(8,128)} %bitcast.2) | data formatting | bytes 9437184
